TPU v7x, 32 devices: a whole 2x2x4 slice. The times are simulated.
32 devices in a mesh: lat: 8 (over z, y), lon: 4 (over x, core).
Axes of the slice: x: 2, y: 2, z: 4, core: 2. Of those that a mesh axis runs over, the one named last changes fastest.
Arguments:
- field: bfloat16 [150, 128, 1024], P(None, 'lat', 'lon'), may hold values from -6 to 6
- land_mask: int32 [128, 1024], P('lat', 'lon'), may hold values 0 or 1
- fold_partner: int32 [1024], replicated, may hold values from 0 to 1023, as said below
- dw_kernel: float32 [150, 7, 7], replicated, may hold values from -0.875 to 0.875
- norm_gain: float32 [150], replicated, may hold values from 0.1 to 1.9
- w_in: bfloat16 [150, 600], replicated, may hold values from -0.5 to 0.5
- w_out: bfloat16 [600, 150], replicated, may hold values from -0.25 to 0.25
- spec_gain: float32 [2, 150, 512], replicated, may hold values from -12 to 12
- mix_weight: bfloat16 [150, 150], replicated, may hold values from -0.5 to 0.5
Outputs:
- block_out: bfloat16 [150, 128, 1024], P(None, 'lat', 'lon')
Inputs may be any that keep to these rules, and one draw needn't show every extreme that they name: There is one s such that fold_partner[j] = (s - j) mod 1024 for every j.
All inputs are finite; a program needn't handle non-finite values. No bound on the sum of `land_mask` on one device may be relied on, other than what follows from the above.
Results may differ from a plain program's by a relative error of at most 0.0065.
Values may be sent and summed in bfloat16 or wider, within the bound.
A program may use at most 128 MiB of HBM per device.

v0:
```python
import math
import jax
import jax.numpy as jnp
from jax import lax
from jax.sharding import PartitionSpec as P


def extended_2(cells, sides, width, closed):
    for axis, dim in sides:
        count = lax.axis_size(axis)
        ends = count if closed else count - 1
        head = lax.slice_in_dim(cells, 0, width, axis=dim)
        tail = lax.slice_in_dim(cells, cells.shape[dim] - width, cells.shape[dim], axis=dim)
        cells = jnp.concatenate(
            [
                lax.ppermute(tail, axis, [(i, (i + 1) % count) for i in range(ends)]),
                cells,
                lax.ppermute(head, axis, [((i + 1) % count, i) for i in range(ends)]),
            ],
            axis=dim,
        )
    return cells


def dft_table(lon_points, mode_count, col_count):
    points = jnp.arange(col_count, dtype=jnp.int32)
    freqs = jnp.arange(mode_count, dtype=jnp.int32)
    phase_index = points[:, None] * freqs[None, :] % lon_points
    angles = phase_index.astype(jnp.float32) * (2.0 * math.pi / lon_points)
    factor = 1.0 / math.sqrt(lon_points)
    return jnp.concatenate([jnp.cos(angles) * factor, -jnp.sin(angles) * factor], axis=1).astype(
        jnp.bfloat16
    )


def apply_gain(spectrum, spec_gain, mode_count):
    spec_re = spectrum[..., :mode_count]
    spec_im = spectrum[..., mode_count:]
    gain_re = spec_gain[0][:, None, :]
    gain_im = spec_gain[1][:, None, :]
    return jnp.concatenate(
        [gain_re * spec_re - gain_im * spec_im, gain_re * spec_im + gain_im * spec_re], axis=-1
    ).astype(jnp.bfloat16)


def depthwise_conv(extended, dw_kernel, lat_rows, lon_cols):
    total = jnp.zeros((extended.shape[0], lat_rows, lon_cols), jnp.float32)
    for tap_row in range(7):
        for tap_col in range(7):
            weight_col = dw_kernel[:, tap_row, tap_col][:, None, None]
            total = total + weight_col * extended[
                :, tap_row : tap_row + lat_rows, tap_col : tap_col + lon_cols
            ].astype(jnp.float32)
    return total


def point_mixer(depth, masked, wet_grid, norm_gain, w_in, w_out):
    channels = depth.shape[0]
    flat = depth.reshape(channels, -1)
    average = jnp.mean(flat, axis=0, keepdims=True)
    centred = flat - average
    variance = jnp.mean(centred * centred, axis=0, keepdims=True)
    normed = (centred * lax.rsqrt(variance + 1e-06) * norm_gain[:, None]).astype(jnp.bfloat16)
    pre_act = jnp.einsum("ch,cp->hp", w_in, normed, preferred_element_type=jnp.float32)
    hidden = jax.nn.gelu(pre_act, approximate=True).astype(jnp.bfloat16)
    branch = jnp.einsum("hc,hp->cp", w_out, hidden, preferred_element_type=jnp.float32)
    wet_flat = wet_grid.reshape(1, -1).astype(jnp.float32)
    result = wet_flat * (masked.reshape(channels, -1).astype(jnp.float32) + branch)
    return result.astype(jnp.bfloat16).reshape(depth.shape)


def local(field, land_mask, fold_partner, dw_kernel, norm_gain, w_in, w_out, spec_gain, mix_weight):
    channels, lat_rows, lon_cols = field.shape
    lat_count = lax.axis_size("lat")
    lon_count = lax.axis_size("lon")
    lon_points = lon_cols * lon_count
    mode_count = spec_gain.shape[2]
    wet_grid = land_mask.astype(field.dtype)
    masked = field * wet_grid[None]
    top_rows = masked[:, lat_rows - 3 :, :][:, ::-1, :]
    fold_full = lax.all_gather(top_rows, "lon", axis=2, tiled=True)
    lon_first = lax.axis_index("lon") * lon_cols
    window = (lon_first - 3 + jnp.arange(lon_cols + 6, dtype=jnp.int32)) % lon_points
    ghost_rows = jnp.take(fold_full, jnp.take(fold_partner, window), axis=2)
    lat_index = lax.axis_index("lat")
    lon_padded = extended_2(masked, (("lon", 2),), 3, True)
    padded = extended_2(lon_padded, (("lat", 1),), 3, False)
    south_rows = padded[:, :3]
    north_rows = jnp.where(lat_index == lat_count - 1, ghost_rows, padded[:, lat_rows + 3 :])
    extended = jnp.concatenate([south_rows, padded[:, 3 : lat_rows + 3], north_rows], axis=1)
    depth = depthwise_conv(extended, dw_kernel, lat_rows, lon_cols)
    group_rows = math.gcd(lat_rows, 8)

    def mix_rows(group_index, result):
        offset = group_index * group_rows
        mixed_block = point_mixer(
            lax.dynamic_slice_in_dim(depth, offset, group_rows, 1),
            lax.dynamic_slice_in_dim(masked, offset, group_rows, 1),
            lax.dynamic_slice_in_dim(wet_grid, offset, group_rows, 0),
            norm_gain,
            w_in,
            w_out,
        )
        return lax.dynamic_update_slice_in_dim(result, mixed_block, offset, 1)

    residual = lax.fori_loop(
        0, lat_rows // group_rows, mix_rows, jnp.zeros(field.shape, jnp.bfloat16)
    )
    by_rows = lax.all_to_all(residual, "lon", split_axis=1, concat_axis=2, tiled=True)
    row_count = by_rows.shape[1]
    fourier = dft_table(lon_points, mode_count, lon_points)
    spectrum = jnp.dot(
        by_rows.reshape(channels * row_count, lon_points),
        fourier,
        preferred_element_type=jnp.float32,
    )
    scaled = apply_gain(
        spectrum.reshape(channels, row_count, 2 * mode_count), spec_gain, mode_count
    )
    along_rows = jnp.einsum(
        "crk,nk->crn", scaled, fourier, preferred_element_type=jnp.float32
    ).astype(jnp.bfloat16)
    spatial = lax.all_to_all(along_rows, "lon", split_axis=2, concat_axis=1, tiled=True)
    mixed = jnp.einsum(
        "cd,cp->dp", mix_weight, spatial.reshape(channels, -1), preferred_element_type=jnp.float32
    )
    wet_flat = wet_grid.reshape(1, -1).astype(jnp.float32)
    output = wet_flat * (residual.reshape(channels, -1).astype(jnp.float32) + mixed)
    return output.astype(jnp.bfloat16).reshape(field.shape)


def solution(mesh):
    placed = (P(None, "lat", "lon"), P("lat", "lon"), P(), P(), P(), P(), P(), P(), P())
    return jax.shard_map(
        local, mesh=mesh, in_specs=placed, out_specs=P(None, "lat", "lon"), check_vma=False
    )
```

profile of v0, /device:TPU:24, one launch (start us, length us, event | category | flops | bytes accessed | tf_op | source)
XLA Modules:
  0.0 204.7 jit_solution(11672251696216430919)
XLA Ops:
  0.9 4.5 %copy.33 = bf16[150,16,256]{0,1,2:T(8,128)(2,1)} copy(bf16[150,16,256]{2,1,0:T(8,128)(2,1)} %param.11) | data formatting | bytes 2457600 | tf_op args[0]
  5.4 1.9 broadcast_multiply_fusion.1
  8.0 1.7 collective-permute-start.1
  11.3 1.2 rev.3
  12.7 9.4 %all_gather.3 = bf16[150,3,1024]{2,0,1:T(8,128)(2,1)S(1)} all-gather(bf16[150,3,256]{2,0,1:T(8,128)(2,1)S(1)} %copy.36), channel_id=1, replica_groups=mesh['lat'=8,'lon'=4] {'lon'}, dimensions={2}, use_global_device_ids=true | all-gather | bytes 1152000 | tf_op jit(solution)/shard_map/all_gather | solution.py:81
  22.2 1.7 gather_fusion
  24.5 1.5 pad_maximum_fusion.5
  25.9 1.4 copy.38
  27.3 3.3 %collective-permute-start.3 = (bf16[150,3,262]{2,0,1:T(8,128)(2,1)S(1)}, bf16[150,3,262]{2,0,1:T(8,128)(2,1)}, u32[]{:S(2)}, u32[]{:S(2)}) collective-permute-start(bf16[150,3,262]{2,0,1:T(8,128)(2,1)S(1)} %copy.38), channel_id=1, source_target_pairs={{4,0},{8,4},{12,8},{16,12},{20,16},{24,20},{28,24},{5,1},{9,5},{13... | collective-permute-start | bytes 707408 | tf_op jit(solution)/shard_map/ppermute | solution.py:18
  30.7 3.2 %copy.40 = bf16[150,16,256]{2,1,0:T(8,128)(2,1)} copy(bf16[150,16,256]{0,1,2:T(8,128)(2,1)S(1)} %broadcast_multiply_fusion.1) | data formatting | bytes 2457600 | tf_op jit(solution)/shard_map/while | solution.py:106
  33.9 2.5 %copy.37 = bf16[150,3,1024]{0,1,2:T(4,128)(2,1)} copy(bf16[150,3,1024]{2,0,1:T(8,128)(2,1)S(1)} %all_gather.3) | data formatting | bytes 1843200 | tf_op jit(solution)/shard_map/all_gather | solution.py:81
  36.4 3.6 %gather_fusion.1 = bf16[262,150,3]{1,2,0:T(4,128)(2,1)} fusion(bf16[150,3,1024]{0,1,2:T(4,128)(2,1)} %copy.37, s32[1024]{0:T(1024)S(1)} %pad_clamp_fusion), kind=kCustom, calls=%fused_computation.1 | custom fusion | bytes 472648 | tf_op jit(solution)/shard_map/jit(_take)/gather | solution.py:84
  40.0 1.6 fusion.48
  41.6 2.1 %copy.34 = bf16[150,3,262]{2,0,1:T(8,128)(2,1)} copy(bf16[150,3,262]{0,1,2:T(4,128)(2,1)} %get-tuple-element.195) | data formatting | bytes 471600 | tf_op jit(solution)/shard_map/slice | solution.py:13
  43.7 3.4 %collective-permute-start.2 = (bf16[150,3,262]{2,0,1:T(8,128)(2,1)}, bf16[150,3,262]{2,0,1:T(8,128)(2,1)}, u32[]{:S(2)}, u32[]{:S(2)}) collective-permute-start(bf16[150,3,262]{2,0,1:T(8,128)(2,1)} %copy.34), channel_id=1, source_target_pairs={{0,4},{4,8},{8,12},{12,16},{16,20},{20,24},{24,28},{1,5},{5,9},{9,... | collective-permute-start | bytes 707408 | tf_op jit(solution)/shard_map/ppermute | solution.py:16
  47.1 1.3 copy.39
  48.5 2.0 bitcast_select_fusion
  50.5 6.5 %collective-permute-done.2 = bf16[150,3,262]{2,0,1:T(8,128)(2,1)} collective-permute-done((bf16[150,3,262]{2,0,1:T(8,128)(2,1)}, bf16[150,3,262]{2,0,1:T(8,128)(2,1)}, u32[]{:S(2)}, u32[]{:S(2)}) %collective-permute-start.2) | collective-permute-done | bytes 235832 | tf_op jit(solution)/shard_map/ppermute | solution.py:16
  57.0 1.3 copy.35
  58.7 5.1 %maximum_maximum_fusion = (bf16[150,19,262]{0,1,2:T(8,128)(2,1)S(1)}, bf16[150,19,262]{0,1,2:T(8,128)(2,1)S(1)}) fusion(bf16[150,16,3]{0,1,2:T(8,128)(2,1)S(1)} %collective-permute-done.1, bf16[150,16,256]{0,1,2:T(8,128)(2,1)S(1)} %broadcast_multiply_fusion.1, bf16[150,16,3]{0,1,2:T(8,128)(2,1)S(1)} %collective-permute-done, ...), kind=kLoop, calls=%fused_computation.36 | loop fusion | flops 11947200 | bytes 4716000 | tf_op jit(solution)/shard_map/concatenate | solution.py:90
  64.2 41.2 %multiply_add_fusion = f32[150,16,256]{0,1,2:T(8,128)} fusion(bf16[150,16,256]{0,1,2:T(8,128)(2,1)S(1)} %broadcast_multiply_fusion.1, bf16[150,16,3]{0,1,2:T(8,128)(2,1)S(1)} %collective-permute-done.1, bf16[150,16,3]{0,1,2:T(8,128)(2,1)S(1)} %collective-permute-done, bf16[150,19,262]{0,1,2:T(8,128)(2,1)S(1)} %get-tuple-element.194, ...), kind=kLoop, calls=%fused_computation.35 | loop fusion | flops 93388800 | bytes 55354200 | tf_op jit(solution)/shard_map/add | solution.py:51
  105.5 5.2 %copy.41 = f32[150,16,256]{2,1,0:T(8,128)} copy(f32[150,16,256]{0,1,2:T(8,128)} %multiply_add_fusion) | data formatting | bytes 4915200 | tf_op jit(solution)/shard_map/while | solution.py:106
  110.6 1.1 broadcast_in_dim.33
  111.7 16.3 %while.13 = (s32[]{:T(128)}, bf16[150,16,256]{2,1,0:T(8,128)(2,1)}, bf16[16,256]{1,0:T(8,128)(2,1)S(1)}, bf16[150,16,256]{2,1,0:T(8,128)(2,1)}, f32[150,16,256]{...) while((s32[]{:T(128)}, bf16[150,16,256]{2,1,0:T(8,128)(2,1)}, ...), condition=%wide.region_3.4_spmd, body=%wide.region_0.3_spmd.sunk | while | flops 752029696 | bytes 21516636 | solution.py:106
  111.7 1.5 fusion.63
  114.0 1.2 dynamic-slice_convert_fusion.2
  115.7 3.1 %fusion.65 = bf16[150,2048]{1,0:T(8,128)(2,1)S(1)} fusion(f32[150,2048]{1,0:T(8,128)S(1)} %bitcast.157, bf16[600,150]{0,1:T(8,128)(2,1)} %get-tuple-element.344, bf16[150,600]{1,0:T(8,128)(2,1)S(1)} %get-tuple-element.343, f32[150,2048]{1,0:T(8,128)S(1)} %bitcast.156, f32[150]{0:T(256)S(1)} %get-tuple-element.342, f32[2048]{0:T(1024)S(1)} %bitcast.165, ...), kind=kOutput, calls=%fused_computation.14.clone.1 | convolution fusion | flops 750489600 | bytes 3457176 | tf_op jit(solution)/shard_map/while/body/eval_jaxpr/hc,hp->cp/dot_general | solution.py:66
  119.0 0.9 slice_dynamic-update-slice_fusion.2
  119.9 1.5 fusion.63
  122.2 1.2 dynamic-slice_convert_fusion.2
  123.9 3.1 %fusion.65 = bf16[150,2048]{1,0:T(8,128)(2,1)S(1)} fusion(f32[150,2048]{1,0:T(8,128)S(1)} %bitcast.157, bf16[600,150]{0,1:T(8,128)(2,1)} %get-tuple-element.344, bf16[150,600]{1,0:T(8,128)(2,1)S(1)} %get-tuple-element.343, f32[150,2048]{1,0:T(8,128)S(1)} %bitcast.156, f32[150]{0:T(256)S(1)} %get-tuple-element.342, f32[2048]{0:T(1024)S(1)} %bitcast.165, ...), kind=kOutput, calls=%fused_computation.14.clone.1 | convolution fusion | flops 750489600 | bytes 3457176 | tf_op jit(solution)/shard_map/while/body/eval_jaxpr/hc,hp->cp/dot_general | solution.py:66
  127.2 0.9 slice_dynamic-update-slice_fusion.2
  128.1 2.8 %copy.43 = bf16[150,16,256]{2,0,1:T(8,128)(2,1)} copy(bf16[150,16,256]{2,1,0:T(8,128)(2,1)} %get-tuple-element.144) | data formatting | bytes 2457600 | tf_op jit(solution)/shard_map/while | solution.py:106
  130.9 3.8 %all-to-all-start = ((bf16[150,16,256]{2,0,1:T(8,128)(2,1)}), bf16[150,16,256]{2,0,1:T(8,128)(2,1)S(1)}, u32[]{:S(2)}, u32[]{:S(2)}) async-start(bf16[150,16,256]{2,0,1:T(8,128)(2,1)} %copy.43), calls=%async_computation | async-start | bytes 2490368 | tf_op jit(solution)/shard_map/all_to_all | solution.py:109
  135.2 9.3 %multiply_convert_fusion.3 = (bf16[1024,512]{1,0:T(8,128)(2,1)}, bf16[1024,512]{1,0:T(8,128)(2,1)}) fusion(), kind=kLoop, calls=%fused_computation.55 | loop fusion | flops 9961472 | bytes 2097152 | tf_op jit(solution)/shard_map/convert.7
  144.6 6.4 %all-to-all-done = bf16[150,16,256]{2,0,1:T(8,128)(2,1)S(1)} async-done(((bf16[150,16,256]{2,0,1:T(8,128)(2,1)}), bf16[150,16,256]{2,0,1:T(8,128)(2,1)S(1)}, u32[]{:S(2)}, u32[]{:S(2)}) %all-to-all-start) | async-done | bytes 1228832 | tf_op jit(solution)/shard_map/all_to_all | solution.py:109
  151.0 1.0 copy.65
  151.9 0.8 dot_general.27
  152.7 3.0 %fusion.35 = f32[150,4,1024]{2,0,1:T(8,128)S(1)} fusion(bf16[150,4,1024]{2,0,1:T(8,128)(2,1)S(1)} %dot_general.27, bf16[1024,512]{1,0:T(8,128)(2,1)} %get-tuple-element.250, bf16[1024,512]{1,0:T(8,128)(2,1)} %get-tuple-element.251), kind=kOutput, calls=%fused_computation.61 | convolution fusion | flops 1262485504 | bytes 5783552 | tf_op jit(solution)/shard_map/dot_general | solution.py:112
  157.2 1.5 convolution_convert_fusion
  158.8 2.5 %copy.46 = bf16[150,4,1024]{0,1,2:T(4,128)(2,1)} copy(bf16[150,4,1024]{2,0,1:T(8,128)(2,1)S(1)} %convolution_convert_fusion) | data formatting | bytes 2457600 | tf_op jit(solution)/shard_map/convert_element_type | solution.py:122
  161.3 4.5 %all-to-all-start.1 = ((bf16[150,4,1024]{0,1,2:T(4,128)(2,1)}), bf16[150,4,1024]{0,1,2:T(4,128)(2,1)}, u32[]{:S(2)}, u32[]{:S(2)}) async-start(bf16[150,4,1024]{0,1,2:T(4,128)(2,1)} %copy.46), calls=%async_computation.1 | async-start | bytes 4194304 | tf_op jit(solution)/shard_map/all_to_all | solution.py:123
  166.1 2.0 copy.60
  168.2 23.3 %all-to-all-done.1 = bf16[150,4,1024]{0,1,2:T(4,128)(2,1)} async-done(((bf16[150,4,1024]{0,1,2:T(4,128)(2,1)}), bf16[150,4,1024]{0,1,2:T(4,128)(2,1)}, u32[]{:S(2)}, u32[]{:S(2)}) %all-to-all-start.1) | async-done | bytes 1228832 | tf_op jit(solution)/shard_map/all_to_all | solution.py:123
  191.5 6.3 %copy.48 = bf16[150,4,4,256]{3,2,1,0:T(4,128)(2,1)} copy(bf16[150,4,4,256]{0,2,3,1:T(4,128)(2,1)} %bitcast.59) | data formatting | bytes 2457600 | tf_op jit(solution)/shard_map/all_to_all | solution.py:123
  197.8 3.5 %reshape.188 = bf16[150,4096]{1,0:T(8,128)(2,1)} reshape(bf16[150,4,4,256]{3,2,1,0:T(4,128)(2,1)} %copy.48) | data formatting | bytes 2457600 | tf_op jit(solution)/shard_map/reshape | solution.py:125
  201.3 1.9 fusion.24
  203.5 1.1 slice.532
  (144 shorter events, 9.7 us)
Async XLA Ops:
  0.0 201.3 %copy-start = (bf16[150,150]{1,0:T(8,128)(2,1)S(1)}, bf16[150,150]{1,0:T(8,128)(2,1)}, u32[]{:S(2)}) copy-start(bf16[150,150]{1,0:T(8,128)(2,1)} %param.19) | copy-start | bytes 135004
  0.9 9.1 %copy-start.6 = (f32[150,7,7]{0,2,1:T(8,128)S(1)}, f32[150,7,7]{0,2,1:T(8,128)}, u32[]{:S(2)}) copy-start(f32[150,7,7]{0,2,1:T(8,128)} %param.14) | copy-start | bytes 88204
  5.4 16.8 %copy-start.1 = (s32[1024]{0:T(1024)S(1)}, s32[1024]{0:T(1024)}, u32[]{:S(2)}) copy-start(s32[1024]{0:T(1024)} %param.13) | copy-start | bytes 12292
  8.0 16.5 %collective-permute-start = (bf16[150,16,3]{0,1,2:T(8,128)(2,1)}, bf16[150,16,3]{0,1,2:T(8,128)(2,1)S(1)}, u32[]{:S(2)}, u32[]{:S(2)}) collective-permute-start(bf16[150,16,3]{0,1,2:T(8,128)(2,1)} %get-tuple-element.197), channel_id=1, source_target_pairs={{0,1},{1,2},{2,3},{3,0},{4,5},{5,6},{6,7},{7,4},{8,9},{9,10},{10,1... | collective-permute-start | bytes 43208 | tf_op jit(solution)/shard_map/ppermute | solution.py:16
  8.0 16.5 %collective-permute-start.1 = (bf16[150,16,3]{0,1,2:T(8,128)(2,1)}, bf16[150,16,3]{0,1,2:T(8,128)(2,1)S(1)}, u32[]{:S(2)}, u32[]{:S(2)}) collective-permute-start(bf16[150,16,3]{0,1,2:T(8,128)(2,1)} %get-tuple-element.198), channel_id=1, source_target_pairs={{1,0},{2,1},{3,2},{0,3},{5,4},{6,5},{7,6},{4,7},{9,8},{10,9},{11,1... | collective-permute-start | bytes 43208 | tf_op jit(solution)/shard_map/ppermute | solution.py:18
  27.3 19.8 %collective-permute-start.3 = (bf16[150,3,262]{2,0,1:T(8,128)(2,1)S(1)}, bf16[150,3,262]{2,0,1:T(8,128)(2,1)}, u32[]{:S(2)}, u32[]{:S(2)}) collective-permute-start(bf16[150,3,262]{2,0,1:T(8,128)(2,1)S(1)} %copy.38), channel_id=1, source_target_pairs={{4,0},{8,4},{12,8},{16,12},{20,16},{24,20},{28,24},{5,1},{9,5},{13... | collective-permute-start | bytes 707408 | tf_op jit(solution)/shard_map/ppermute | solution.py:18
  30.7 17.8 %copy-start.46 = (pred[262]{0:T(512)(128)(4,1)S(1)}, pred[262]{0:T(512)(128)(4,1)}, u32[]{:S(2)}) copy-start(pred[262]{0:T(512)(128)(4,1)} %compare_and_fusion) | copy-start | bytes 790
  43.7 13.3 %collective-permute-start.2 = (bf16[150,3,262]{2,0,1:T(8,128)(2,1)}, bf16[150,3,262]{2,0,1:T(8,128)(2,1)}, u32[]{:S(2)}, u32[]{:S(2)}) collective-permute-start(bf16[150,3,262]{2,0,1:T(8,128)(2,1)} %copy.34), channel_id=1, source_target_pairs={{0,4},{4,8},{8,12},{12,16},{16,20},{20,24},{24,28},{1,5},{5,9},{9,... | collective-permute-start | bytes 707408 | tf_op jit(solution)/shard_map/ppermute | solution.py:16
  58.3 5.5 %copy-start.7 = (f32[150,1,1]{0,2,1:T(1,128)S(1)}, f32[150,1,1]{0,2,1:T(1,128)}, u32[]{:S(2)}) copy-start(f32[150,1,1]{0,2,1:T(1,128)} %get-tuple-element.223) | copy-start | bytes 1804
  58.3 5.5 %copy-start.8 = (f32[150,1,1]{0,2,1:T(1,128)S(1)}, f32[150,1,1]{0,2,1:T(1,128)}, u32[]{:S(2)}) copy-start(f32[150,1,1]{0,2,1:T(1,128)} %get-tuple-element.224) | copy-start | bytes 1804
  58.4 5.5 %copy-start.9 = (f32[150,1,1]{0,2,1:T(1,128)S(1)}, f32[150,1,1]{0,2,1:T(1,128)}, u32[]{:S(2)}) copy-start(f32[150,1,1]{0,2,1:T(1,128)} %get-tuple-element.225) | copy-start | bytes 1804
  58.4 5.5 %copy-start.10 = (f32[150,1,1]{0,2,1:T(1,128)S(1)}, f32[150,1,1]{0,2,1:T(1,128)}, u32[]{:S(2)}) copy-start(f32[150,1,1]{0,2,1:T(1,128)} %get-tuple-element.226) | copy-start | bytes 1804
  58.4 5.5 %copy-start.11 = (f32[150,1,1]{0,2,1:T(1,128)S(1)}, f32[150,1,1]{0,2,1:T(1,128)}, u32[]{:S(2)}) copy-start(f32[150,1,1]{0,2,1:T(1,128)} %get-tuple-element.227) | copy-start | bytes 1804
  58.4 5.5 %copy-start.12 = (f32[150,1,1]{0,2,1:T(1,128)S(1)}, f32[150,1,1]{0,2,1:T(1,128)}, u32[]{:S(2)}) copy-start(f32[150,1,1]{0,2,1:T(1,128)} %get-tuple-element.228) | copy-start | bytes 1804
  58.4 5.5 %copy-start.13 = (f32[150,1,1]{0,2,1:T(1,128)S(1)}, f32[150,1,1]{0,2,1:T(1,128)}, u32[]{:S(2)}) copy-start(f32[150,1,1]{0,2,1:T(1,128)} %get-tuple-element.229) | copy-start | bytes 1804
  58.4 5.5 %copy-start.14 = (f32[150,1,1]{0,2,1:T(1,128)S(1)}, f32[150,1,1]{0,2,1:T(1,128)}, u32[]{:S(2)}) copy-start(f32[150,1,1]{0,2,1:T(1,128)} %get-tuple-element.230) | copy-start | bytes 1804
  58.4 5.5 %copy-start.15 = (f32[150,1,1]{0,2,1:T(1,128)S(1)}, f32[150,1,1]{0,2,1:T(1,128)}, u32[]{:S(2)}) copy-start(f32[150,1,1]{0,2,1:T(1,128)} %get-tuple-element.231) | copy-start | bytes 1804
  58.4 5.5 %copy-start.16 = (f32[150,1,1]{0,2,1:T(1,128)S(1)}, f32[150,1,1]{0,2,1:T(1,128)}, u32[]{:S(2)}) copy-start(f32[150,1,1]{0,2,1:T(1,128)} %get-tuple-element.232) | copy-start | bytes 1804
  58.4 5.5 %copy-start.17 = (f32[150,1,1]{0,2,1:T(1,128)S(1)}, f32[150,1,1]{0,2,1:T(1,128)}, u32[]{:S(2)}) copy-start(f32[150,1,1]{0,2,1:T(1,128)} %get-tuple-element.233) | copy-start | bytes 1804
  58.4 5.5 %copy-start.18 = (f32[150,1,1]{0,2,1:T(1,128)S(1)}, f32[150,1,1]{0,2,1:T(1,128)}, u32[]{:S(2)}) copy-start(f32[150,1,1]{0,2,1:T(1,128)} %get-tuple-element.234) | copy-start | bytes 1804
  58.5 5.5 %copy-start.19 = (f32[150,1,1]{0,2,1:T(1,128)S(1)}, f32[150,1,1]{0,2,1:T(1,128)}, u32[]{:S(2)}) copy-start(f32[150,1,1]{0,2,1:T(1,128)} %get-tuple-element.235) | copy-start | bytes 1804
  58.5 5.5 %copy-start.20 = (f32[150,1,1]{0,2,1:T(1,128)S(1)}, f32[150,1,1]{0,2,1:T(1,128)}, u32[]{:S(2)}) copy-start(f32[150,1,1]{0,2,1:T(1,128)} %get-tuple-element.236) | copy-start | bytes 1804
  58.5 5.5 %copy-start.21 = (f32[150,1,1]{0,2,1:T(1,128)S(1)}, f32[150,1,1]{0,2,1:T(1,128)}, u32[]{:S(2)}) copy-start(f32[150,1,1]{0,2,1:T(1,128)} %get-tuple-element.237) | copy-start | bytes 1804
  58.5 5.5 %copy-start.22 = (f32[150,1,1]{0,2,1:T(1,128)S(1)}, f32[150,1,1]{0,2,1:T(1,128)}, u32[]{:S(2)}) copy-start(f32[150,1,1]{0,2,1:T(1,128)} %get-tuple-element.238) | copy-start | bytes 1804
  58.5 5.5 %copy-start.23 = (f32[150,1,1]{0,2,1:T(1,128)S(1)}, f32[150,1,1]{0,2,1:T(1,128)}, u32[]{:S(2)}) copy-start(f32[150,1,1]{0,2,1:T(1,128)} %get-tuple-element.239) | copy-start | bytes 1804
  58.5 5.5 %copy-start.24 = (f32[150,1,1]{0,2,1:T(1,128)S(1)}, f32[150,1,1]{0,2,1:T(1,128)}, u32[]{:S(2)}) copy-start(f32[150,1,1]{0,2,1:T(1,128)} %get-tuple-element.240) | copy-start | bytes 1804
  58.5 5.5 %copy-start.25 = (f32[150,1,1]{0,2,1:T(1,128)S(1)}, f32[150,1,1]{0,2,1:T(1,128)}, u32[]{:S(2)}) copy-start(f32[150,1,1]{0,2,1:T(1,128)} %get-tuple-element.241) | copy-start | bytes 1804
  58.5 5.5 %copy-start.26 = (f32[150,1,1]{0,2,1:T(1,128)S(1)}, f32[150,1,1]{0,2,1:T(1,128)}, u32[]{:S(2)}) copy-start(f32[150,1,1]{0,2,1:T(1,128)} %get-tuple-element.242) | copy-start | bytes 1804
  58.5 5.5 %copy-start.27 = (f32[150,1,1]{0,2,1:T(1,128)S(1)}, f32[150,1,1]{0,2,1:T(1,128)}, u32[]{:S(2)}) copy-start(f32[150,1,1]{0,2,1:T(1,128)} %get-tuple-element.243) | copy-start | bytes 1804
  58.5 5.5 %copy-start.28 = (f32[150,1,1]{0,2,1:T(1,128)S(1)}, f32[150,1,1]{0,2,1:T(1,128)}, u32[]{:S(2)}) copy-start(f32[150,1,1]{0,2,1:T(1,128)} %get-tuple-element.244) | copy-start | bytes 1804
  58.6 5.5 %copy-start.29 = (f32[150,1,1]{0,2,1:T(1,128)S(1)}, f32[150,1,1]{0,2,1:T(1,128)}, u32[]{:S(2)}) copy-start(f32[150,1,1]{0,2,1:T(1,128)} %get-tuple-element.245) | copy-start | bytes 1804
  58.6 5.5 %copy-start.30 = (f32[150,1,1]{0,2,1:T(1,128)S(1)}, f32[150,1,1]{0,2,1:T(1,128)}, u32[]{:S(2)}) copy-start(f32[150,1,1]{0,2,1:T(1,128)} %get-tuple-element.246) | copy-start | bytes 1804
  58.6 5.5 %copy-start.31 = (f32[150,1,1]{0,2,1:T(1,128)S(1)}, f32[150,1,1]{0,2,1:T(1,128)}, u32[]{:S(2)}) copy-start(f32[150,1,1]{0,2,1:T(1,128)} %get-tuple-element.247) | copy-start | bytes 1804
  58.6 5.5 %copy-start.32 = (f32[150,1,1]{0,2,1:T(1,128)S(1)}, f32[150,1,1]{0,2,1:T(1,128)}, u32[]{:S(2)}) copy-start(f32[150,1,1]{0,2,1:T(1,128)} %get-tuple-element.248) | copy-start | bytes 1804
  58.6 5.5 %copy-start.33 = (f32[150,1,1]{0,2,1:T(1,128)S(1)}, f32[150,1,1]{0,2,1:T(1,128)}, u32[]{:S(2)}) copy-start(f32[150,1,1]{0,2,1:T(1,128)} %get-tuple-element.249) | copy-start | bytes 1804
  58.6 5.5 %copy-start.34 = (f32[150,1,1]{0,2,1:T(1,128)S(1)}, f32[150,1,1]{0,2,1:T(1,128)}, u32[]{:S(2)}) copy-start(f32[150,1,1]{0,2,1:T(1,128)} %get-tuple-element.201) | copy-start | bytes 1804
  58.6 5.5 %copy-start.35 = (f32[150,1,1]{0,2,1:T(1,128)S(1)}, f32[150,1,1]{0,2,1:T(1,128)}, u32[]{:S(2)}) copy-start(f32[150,1,1]{0,2,1:T(1,128)} %get-tuple-element.202) | copy-start | bytes 1804
  58.6 5.5 %copy-start.36 = (f32[150,1,1]{0,2,1:T(1,128)S(1)}, f32[150,1,1]{0,2,1:T(1,128)}, u32[]{:S(2)}) copy-start(f32[150,1,1]{0,2,1:T(1,128)} %get-tuple-element.203) | copy-start | bytes 1804
  58.6 5.5 %copy-start.37 = (f32[150,1,1]{0,2,1:T(1,128)S(1)}, f32[150,1,1]{0,2,1:T(1,128)}, u32[]{:S(2)}) copy-start(f32[150,1,1]{0,2,1:T(1,128)} %get-tuple-element.204) | copy-start | bytes 1804
  58.6 5.5 %copy-start.38 = (f32[150,1,1]{0,2,1:T(1,128)S(1)}, f32[150,1,1]{0,2,1:T(1,128)}, u32[]{:S(2)}) copy-start(f32[150,1,1]{0,2,1:T(1,128)} %get-tuple-element.205) | copy-start | bytes 1804
  58.7 5.5 %copy-start.39 = (f32[150,1,1]{0,2,1:T(1,128)S(1)}, f32[150,1,1]{0,2,1:T(1,128)}, u32[]{:S(2)}) copy-start(f32[150,1,1]{0,2,1:T(1,128)} %get-tuple-element.206) | copy-start | bytes 1804
  58.7 5.5 %copy-start.40 = (f32[150,1,1]{0,2,1:T(1,128)S(1)}, f32[150,1,1]{0,2,1:T(1,128)}, u32[]{:S(2)}) copy-start(f32[150,1,1]{0,2,1:T(1,128)} %get-tuple-element.207) | copy-start | bytes 1804
  105.5 6.3 %copy-start.47 = (bf16[150,600]{1,0:T(8,128)(2,1)S(1)}, bf16[150,600]{1,0:T(8,128)(2,1)}, u32[]{:S(2)}) copy-start(bf16[150,600]{1,0:T(8,128)(2,1)} %param.16) | copy-start | bytes 540004
  105.5 6.3 %copy-start.48 = (f32[150]{0:T(256)S(1)}, f32[150]{0:T(256)}, u32[]{:S(2)}) copy-start(f32[150]{0:T(256)} %param.15) | copy-start | bytes 1804
  128.1 6.6 %copy-start.5 = (f32[2,150,512]{2,0,1:T(2,128)S(1)}, f32[2,150,512]{2,0,1:T(2,128)}, u32[]{:S(2)}) copy-start(f32[2,150,512]{2,0,1:T(2,128)} %param.18) | copy-start | bytes 1843204
  130.9 20.0 %all-to-all-start = ((bf16[150,16,256]{2,0,1:T(8,128)(2,1)}), bf16[150,16,256]{2,0,1:T(8,128)(2,1)S(1)}, u32[]{:S(2)}, u32[]{:S(2)}) async-start(bf16[150,16,256]{2,0,1:T(8,128)(2,1)} %copy.43), calls=%async_computation | async-start | bytes 2490368 | tf_op jit(solution)/shard_map/all_to_all | solution.py:109
  158.7 7.0 %copy-start.2 = (bf16[150,16,256]{2,1,0:T(8,128)(2,1)S(1)}, bf16[150,16,256]{2,1,0:T(8,128)(2,1)}, u32[]{:S(2)}) copy-start(bf16[150,16,256]{2,1,0:T(8,128)(2,1)} %get-tuple-element.144) | copy-start | bytes 3686404
  161.3 30.2 %all-to-all-start.1 = ((bf16[150,4,1024]{0,1,2:T(4,128)(2,1)}), bf16[150,4,1024]{0,1,2:T(4,128)(2,1)}, u32[]{:S(2)}, u32[]{:S(2)}) async-start(bf16[150,4,1024]{0,1,2:T(4,128)(2,1)} %copy.46), calls=%async_computation.1 | async-start | bytes 4194304 | tf_op jit(solution)/shard_map/all_to_all | solution.py:123
  (7 other events, 30.3 us)
where the time goes:
time: 206 us; the launch traced here: 205 us
  other arithmetic  68.6 us (33%)
  local copies, waits for them, and re-layouts  60 us (29%)
  waiting for transfers between devices  36.2 us (18%)
  starting transfers between devices  16.7 us (8%)
  matrix products  12.6 us (6%)
  blocking collectives  9.4 us (5%)
    add x1, other arithmetic, depthwise_conv(): total + weight_col * extended[:, tap_row:tap_row + lat_rows, tap_col:tap_...  41.2 us
    all_to_all x1, waiting for transfers between devices, local(): lax.all_to_all(along_rows, 'lon', split_axis=2, concat_axis=1, tiled=True)  23.3 us
    while x3, local copies, waits for them, and re-layouts, local(): lax.fori_loop(0, lat_rows // group_rows, mix_rows, jnp.zeros(field.shape,...  11.2 us
    another operation x2, other arithmetic  9.82 us
    all_gather x1, blocking collectives, local(): fold_full = lax.all_gather(top_rows, 'lon', axis=2, tiled=True)  9.4 us
    unnamed x103, local copies, waits for them, and re-layouts  8.46 us
    ppermute x2, waiting for transfers between devices, extended_2(): lax.ppermute(tail, axis, [(i, (i + 1) % count) for i in range(ends)])  6.5 us
    all_to_all x1, waiting for transfers between devices, local(): lax.all_to_all(residual, 'lon', split_axis=1, concat_axis=2, tiled=True)  6.4 us
  transfers between devices with their start and end apart: 6, of which 3 were waited for; matrix products, arithmetic and copies ran while one was open for 17% of the time, Pallas kernels for 0%

commit v1 on v0

--- a/solution.py
+++ b/solution.py
@@ -120,7 +120,10 @@
     along_rows = jnp.einsum(
         "crk,nk->crn", scaled, fourier, preferred_element_type=jnp.float32
     ).astype(jnp.bfloat16)
-    spatial = lax.all_to_all(along_rows, "lon", split_axis=2, concat_axis=1, tiled=True)
+    count_2 = lax.axis_size("lon")
+    blocks = jnp.stack(jnp.split(along_rows, count_2, axis=2), axis=0)
+    blocks = lax.all_to_all(blocks, "lon", split_axis=0, concat_axis=0)
+    spatial = jnp.concatenate(blocks, axis=1)
     mixed = jnp.einsum(
         "cd,cp->dp", mix_weight, spatial.reshape(channels, -1), preferred_element_type=jnp.float32
     )

time: 206 us -> 192 us (0.932)
  waiting for transfers between devices: 36.2 us -> 26.9 us
  local copies, waits for them, and re-layouts: 60 us -> 55.5 us
    all_to_all x1, waiting for transfers between devices: 23.3 us -> 14 us  [local(): blocks = lax.all_to_all(blocks, 'lon', split_axis=0, concat_axis=0)]
    all_to_all x1 -> x0, local copies, waits for them, and re-layouts: 6.32 us -> none  [local(): lax.all_to_all(along_rows, 'lon', split_axis=2, concat_axis=1, tiled=True)]
    another operation x0 -> x3, local copies, waits for them, and re-layouts: none -> 5.14 us  [the longest x1 3.56 us: local(): spatial.reshape(channels, -1)]
    convert_element_type x1 -> x0, local copies, waits for them, and re-layouts: 2.54 us -> none  [local(): along_rows = jnp.einsum('crk,nk->crn', scaled, fourier, preferred_element...]
    another operation x2 -> x3, other arithmetic: 9.82 us -> 9.98 us
  transfers between devices with their start and end apart: 6 -> 6, of which waited for: 3 -> 3; matrix products, arithmetic and copies ran while one was open for 17% -> 18% of each run, Pallas kernels for 0% -> 0%
where the time goes in v1:
time: 192 us; the launch traced here: 191 us
  other arithmetic  68.9 us (36%)
  local copies, waits for them, and re-layouts  55.5 us (29%)
  waiting for transfers between devices  26.9 us (14%)
  starting transfers between devices  16.5 us (9%)
  matrix products  12.6 us (7%)
  blocking collectives  9.4 us (5%)
    add x1, other arithmetic, depthwise_conv(): total + weight_col * extended[:, tap_row:tap_row + lat_rows, tap_col:tap_...  41.2 us
    all_to_all x1, waiting for transfers between devices, local(): blocks = lax.all_to_all(blocks, 'lon', split_axis=0, concat_axis=0)  14 us
    while x3, local copies, waits for them, and re-layouts, local(): lax.fori_loop(0, lat_rows // group_rows, mix_rows, jnp.zeros(field.shape,...  11.2 us
    another operation x2, other arithmetic  9.82 us
    all_gather x1, blocking collectives, local(): fold_full = lax.all_gather(top_rows, 'lon', axis=2, tiled=True)  9.4 us
    unnamed x103, local copies, waits for them, and re-layouts  8.46 us
    ppermute x2, waiting for transfers between devices, extended_2(): lax.ppermute(tail, axis, [(i, (i + 1) % count) for i in range(ends)])  6.49 us
    all_to_all x1, waiting for transfers between devices, local(): lax.all_to_all(residual, 'lon', split_axis=1, concat_axis=2, tiled=True)  6.4 us
  transfers between devices with their start and end apart: 6, of which 3 were waited for; matrix products, arithmetic and copies ran while one was open for 18% of the time, Pallas kernels for 0%

profile of v1, /device:TPU:24, one launch (start us, length us, event | category | flops | bytes accessed | tf_op | source)
XLA Modules:
  0.0 190.9 jit_solution(7563220064580239137)
XLA Ops:
  0.9 4.5 %copy.32 = bf16[150,16,256]{0,1,2:T(8,128)(2,1)} copy(bf16[150,16,256]{2,1,0:T(8,128)(2,1)} %param.11) | data formatting | bytes 2457600 | tf_op args[0]
  5.4 1.9 %broadcast_multiply_fusion.1 = bf16[150,16,256]{0,1,2:T(8,128)(2,1)S(1)} fusion(bf16[150,16,256]{0,1,2:T(8,128)(2,1)} %copy.32, bf16[16,256]{0,1:T(8,128)(2,1)S(1)} %copy.31), kind=kLoop, calls=%fused_computation.69 | loop fusion | flops 614400 | bytes 2465792 | tf_op jit(solution)/shard_map/mul | solution.py:79
  8.0 1.7 collective-permute-start.1
  11.3 1.2 rev.3
  12.8 9.4 %all_gather.3 = bf16[150,3,1024]{2,0,1:T(8,128)(2,1)S(1)} all-gather(bf16[150,3,256]{2,0,1:T(8,128)(2,1)S(1)} %copy.35), channel_id=1, replica_groups=mesh['lat'=8,'lon'=4] {'lon'}, dimensions={2}, use_global_device_ids=true | all-gather | bytes 1152000 | tf_op jit(solution)/shard_map/all_gather | solution.py:81
  22.2 1.7 gather_fusion
  24.5 1.5 pad_maximum_fusion.6
  26.0 1.4 copy.37
  27.4 3.3 %collective-permute-start.3 = (bf16[150,3,262]{2,0,1:T(8,128)(2,1)S(1)}, bf16[150,3,262]{2,0,1:T(8,128)(2,1)}, u32[]{:S(2)}, u32[]{:S(2)}) collective-permute-start(bf16[150,3,262]{2,0,1:T(8,128)(2,1)S(1)} %copy.37), channel_id=1, source_target_pairs={{4,0},{8,4},{12,8},{16,12},{20,16},{24,20},{28,24},{5,1},{9,5},{13... | collective-permute-start | bytes 707408 | tf_op jit(solution)/shard_map/ppermute | solution.py:18
  30.7 3.2 %copy.39 = bf16[150,16,256]{2,1,0:T(8,128)(2,1)} copy(bf16[150,16,256]{0,1,2:T(8,128)(2,1)S(1)} %broadcast_multiply_fusion.1) | data formatting | bytes 2457600 | tf_op jit(solution)/shard_map/while | solution.py:106
  33.9 2.5 %copy.36 = bf16[150,3,1024]{0,1,2:T(4,128)(2,1)} copy(bf16[150,3,1024]{2,0,1:T(8,128)(2,1)S(1)} %all_gather.3) | data formatting | bytes 1843200 | tf_op jit(solution)/shard_map/all_gather | solution.py:81
  36.4 3.6 %gather_fusion.1 = bf16[262,150,3]{1,2,0:T(4,128)(2,1)} fusion(bf16[150,3,1024]{0,1,2:T(4,128)(2,1)} %copy.36, s32[1024]{0:T(1024)S(1)} %pad_clamp_fusion), kind=kCustom, calls=%fused_computation.1 | custom fusion | bytes 472648 | tf_op jit(solution)/shard_map/jit(_take)/gather | solution.py:84
  40.1 1.6 fusion.48
  41.7 2.1 %copy.33 = bf16[150,3,262]{2,0,1:T(8,128)(2,1)} copy(bf16[150,3,262]{0,1,2:T(4,128)(2,1)} %get-tuple-element.195) | data formatting | bytes 471600 | tf_op jit(solution)/shard_map/slice | solution.py:13
  43.8 3.4 %collective-permute-start.2 = (bf16[150,3,262]{2,0,1:T(8,128)(2,1)}, bf16[150,3,262]{2,0,1:T(8,128)(2,1)}, u32[]{:S(2)}, u32[]{:S(2)}) collective-permute-start(bf16[150,3,262]{2,0,1:T(8,128)(2,1)} %copy.33), channel_id=1, source_target_pairs={{0,4},{4,8},{8,12},{12,16},{16,20},{20,24},{24,28},{1,5},{5,9},{9,... | collective-permute-start | bytes 707408 | tf_op jit(solution)/shard_map/ppermute | solution.py:16
  47.2 1.3 copy.38
  48.6 2.0 %bitcast_select_fusion = bf16[150,3,262]{0,1,2:T(4,128)(2,1)S(1)} fusion(bf16[150,3,262]{0,1,2:T(4,128)(2,1)S(1)} %copy.38, bf16[262,150,3]{1,2,0:T(4,128)(2,1)} %gather_fusion.1, pred[262]{0:T(512)(128)(4,1)S(1)} %copy-done.46, pred[]{:T(512)S(6)} %eq.7), kind=kLoop, calls=%fused_computation.73 | loop fusion | flops 235800 | bytes 707663 | tf_op jit(solution)/shard_map/jit(_where)/select_n | solution.py:89
  50.6 6.5 %collective-permute-done.2 = bf16[150,3,262]{2,0,1:T(8,128)(2,1)} collective-permute-done((bf16[150,3,262]{2,0,1:T(8,128)(2,1)}, bf16[150,3,262]{2,0,1:T(8,128)(2,1)}, u32[]{:S(2)}, u32[]{:S(2)}) %collective-permute-start.2) | collective-permute-done | bytes 235832 | tf_op jit(solution)/shard_map/ppermute | solution.py:16
  57.1 1.3 copy.34
  58.8 5.1 %maximum_maximum_fusion = (bf16[150,19,262]{0,1,2:T(8,128)(2,1)S(1)}, bf16[150,19,262]{0,1,2:T(8,128)(2,1)S(1)}) fusion(bf16[150,16,3]{0,1,2:T(8,128)(2,1)S(1)} %collective-permute-done.1, bf16[150,16,256]{0,1,2:T(8,128)(2,1)S(1)} %broadcast_multiply_fusion.1, bf16[150,16,3]{0,1,2:T(8,128)(2,1)S(1)} %collective-permute-done, ...), kind=kLoop, calls=%fused_computation.36 | loop fusion | flops 11947200 | bytes 4716000 | tf_op jit(solution)/shard_map/concatenate | solution.py:90
  64.3 41.2 %multiply_add_fusion = f32[150,16,256]{0,1,2:T(8,128)} fusion(bf16[150,16,256]{0,1,2:T(8,128)(2,1)S(1)} %broadcast_multiply_fusion.1, bf16[150,16,3]{0,1,2:T(8,128)(2,1)S(1)} %collective-permute-done.1, bf16[150,16,3]{0,1,2:T(8,128)(2,1)S(1)} %collective-permute-done, bf16[150,19,262]{0,1,2:T(8,128)(2,1)S(1)} %get-tuple-element.194, ...), kind=kLoop, calls=%fused_computation.35 | loop fusion | flops 93388800 | bytes 55354200 | tf_op jit(solution)/shard_map/add | solution.py:51
  105.6 5.1 %copy.40 = f32[150,16,256]{2,1,0:T(8,128)} copy(f32[150,16,256]{0,1,2:T(8,128)} %multiply_add_fusion) | data formatting | bytes 4915200 | tf_op jit(solution)/shard_map/while | solution.py:106
  110.7 1.1 broadcast_in_dim.33
  111.8 16.3 %while.13 = (s32[]{:T(128)}, bf16[150,16,256]{2,1,0:T(8,128)(2,1)}, bf16[16,256]{1,0:T(8,128)(2,1)S(1)}, bf16[150,16,256]{2,1,0:T(8,128)(2,1)}, f32[150,16,256]{...) while((s32[]{:T(128)}, bf16[150,16,256]{2,1,0:T(8,128)(2,1)}, ...), condition=%wide.region_3.4_spmd, body=%wide.region_0.3_spmd.sunk | while | flops 752029696 | bytes 21516636 | solution.py:106
  111.8 1.5 fusion.63
  114.1 1.2 dynamic-slice_convert_fusion.2
  115.8 3.1 %fusion.65 = bf16[150,2048]{1,0:T(8,128)(2,1)S(1)} fusion(f32[150,2048]{1,0:T(8,128)S(1)} %bitcast.162, bf16[600,150]{0,1:T(8,128)(2,1)} %get-tuple-element.348, bf16[150,600]{1,0:T(8,128)(2,1)S(1)} %get-tuple-element.347, f32[150,2048]{1,0:T(8,128)S(1)} %bitcast.161, f32[150]{0:T(256)S(1)} %get-tuple-element.346, f32[2048]{0:T(1024)S(1)} %bitcast.170, ...), kind=kOutput, calls=%fused_computation.14.clone.1 | convolution fusion | flops 750489600 | bytes 3457176 | tf_op jit(solution)/shard_map/while/body/eval_jaxpr/hc,hp->cp/dot_general | solution.py:66
  119.1 0.9 slice_dynamic-update-slice_fusion.2
  120.0 1.5 fusion.63
  122.2 1.2 dynamic-slice_convert_fusion.2
  124.0 3.1 %fusion.65 = bf16[150,2048]{1,0:T(8,128)(2,1)S(1)} fusion(f32[150,2048]{1,0:T(8,128)S(1)} %bitcast.162, bf16[600,150]{0,1:T(8,128)(2,1)} %get-tuple-element.348, bf16[150,600]{1,0:T(8,128)(2,1)S(1)} %get-tuple-element.347, f32[150,2048]{1,0:T(8,128)S(1)} %bitcast.161, f32[150]{0:T(256)S(1)} %get-tuple-element.346, f32[2048]{0:T(1024)S(1)} %bitcast.170, ...), kind=kOutput, calls=%fused_computation.14.clone.1 | convolution fusion | flops 750489600 | bytes 3457176 | tf_op jit(solution)/shard_map/while/body/eval_jaxpr/hc,hp->cp/dot_general | solution.py:66
  127.3 0.9 slice_dynamic-update-slice_fusion.2
  128.1 2.8 %copy.42 = bf16[150,16,256]{2,0,1:T(8,128)(2,1)} copy(bf16[150,16,256]{2,1,0:T(8,128)(2,1)} %get-tuple-element.144) | data formatting | bytes 2457600 | tf_op jit(solution)/shard_map/while | solution.py:106
  131.0 3.8 %all-to-all-start = ((bf16[150,16,256]{2,0,1:T(8,128)(2,1)}), bf16[150,16,256]{2,0,1:T(8,128)(2,1)S(1)}, u32[]{:S(2)}, u32[]{:S(2)}) async-start(bf16[150,16,256]{2,0,1:T(8,128)(2,1)} %copy.42), calls=%async_computation | async-start | bytes 2490368 | tf_op jit(solution)/shard_map/all_to_all | solution.py:109
  135.3 9.3 %multiply_convert_fusion.3 = (bf16[1024,512]{1,0:T(8,128)(2,1)}, bf16[1024,512]{1,0:T(8,128)(2,1)}) fusion(), kind=kLoop, calls=%fused_computation.55 | loop fusion | flops 9961472 | bytes 2097152 | tf_op jit(solution)/shard_map/convert.7
  144.6 6.4 %all-to-all-done = bf16[150,16,256]{2,0,1:T(8,128)(2,1)S(1)} async-done(((bf16[150,16,256]{2,0,1:T(8,128)(2,1)}), bf16[150,16,256]{2,0,1:T(8,128)(2,1)S(1)}, u32[]{:S(2)}, u32[]{:S(2)}) %all-to-all-start) | async-done | bytes 1228832 | tf_op jit(solution)/shard_map/all_to_all | solution.py:109
  151.0 1.0 copy.61
  152.0 0.8 dot_general.27
  152.8 3.0 %fusion.35 = f32[150,4,1024]{2,0,1:T(8,128)S(1)} fusion(bf16[150,4,1024]{2,0,1:T(8,128)(2,1)S(1)} %dot_general.27, bf16[1024,512]{1,0:T(8,128)(2,1)} %get-tuple-element.254, bf16[1024,512]{1,0:T(8,128)(2,1)} %get-tuple-element.255), kind=kOutput, calls=%fused_computation.61 | convolution fusion | flops 1262485504 | bytes 5783552 | tf_op jit(solution)/shard_map/dot_general | solution.py:112
  157.3 1.5 convolution_convert_fusion
  159.1 1.5 copy.45
  160.6 4.3 %all-to-all-start.1 = ((bf16[4,150,4,256]{3,2,1,0:T(4,128)(2,1)}), bf16[4,150,4,256]{3,2,1,0:T(4,128)(2,1)}, u32[]{:S(2)}, u32[]{:S(2)}) async-start(bf16[4,150,4,256]{3,2,1,0:T(4,128)(2,1)} %copy.45), calls=%async_computation.1 | async-start | bytes 2457600 | tf_op jit(solution)/shard_map/all_to_all | solution.py:125
  165.3 2.0 %copy.56 = f32[19,8,16,256]{3,1,2,0:T(8,128)S(1)} copy(f32[19,8,16,256]{3,2,1,0:T(8,128)S(1)} %bitcast.165) | data formatting | bytes 4980736
  167.3 14.0 %all-to-all-done.1 = bf16[4,150,4,256]{3,2,1,0:T(4,128)(2,1)} async-done(((bf16[4,150,4,256]{3,2,1,0:T(4,128)(2,1)}), bf16[4,150,4,256]{3,2,1,0:T(4,128)(2,1)}, u32[]{:S(2)}, u32[]{:S(2)}) %all-to-all-start.1) | async-done | bytes 1228832 | tf_op jit(solution)/shard_map/all_to_all | solution.py:125
  181.3 2.7 %copy.46 = bf16[150,4,4,256]{3,2,1,0:T(4,128)(2,1)} copy(bf16[150,4,4,256]{3,2,0,1:T(4,128)(2,1)} %bitcast.61) | data formatting | bytes 2457600 | tf_op jit(solution)/shard_map/reshape | solution.py:126
  184.1 3.6 %reshape_reshape.3 = bf16[150,4096]{1,0:T(8,128)(2,1)} reshape(bf16[150,4,4,256]{3,2,1,0:T(4,128)(2,1)} %copy.46) | data formatting | bytes 2457600 | tf_op jit(solution)/shard_map/reshape;reshape | solution.py:128
  187.6 1.9 fusion.24
  189.8 1.1 slice.532
  (146 shorter events, 10.0 us)
Async XLA Ops:
  0.0 187.6 %copy-start = (bf16[150,150]{1,0:T(8,128)(2,1)S(1)}, bf16[150,150]{1,0:T(8,128)(2,1)}, u32[]{:S(2)}) copy-start(bf16[150,150]{1,0:T(8,128)(2,1)} %param.19) | copy-start | bytes 135004
  0.9 9.1 %copy-start.6 = (f32[150,7,7]{0,2,1:T(8,128)S(1)}, f32[150,7,7]{0,2,1:T(8,128)}, u32[]{:S(2)}) copy-start(f32[150,7,7]{0,2,1:T(8,128)} %param.14) | copy-start | bytes 88204
  5.4 16.8 %copy-start.1 = (s32[1024]{0:T(1024)S(1)}, s32[1024]{0:T(1024)}, u32[]{:S(2)}) copy-start(s32[1024]{0:T(1024)} %param.13) | copy-start | bytes 12292
  8.0 16.6 %collective-permute-start = (bf16[150,16,3]{0,1,2:T(8,128)(2,1)}, bf16[150,16,3]{0,1,2:T(8,128)(2,1)S(1)}, u32[]{:S(2)}, u32[]{:S(2)}) collective-permute-start(bf16[150,16,3]{0,1,2:T(8,128)(2,1)} %get-tuple-element.197), channel_id=1, source_target_pairs={{0,1},{1,2},{2,3},{3,0},{4,5},{5,6},{6,7},{7,4},{8,9},{9,10},{10,1... | collective-permute-start | bytes 43208 | tf_op jit(solution)/shard_map/ppermute | solution.py:16
  8.0 16.6 %collective-permute-start.1 = (bf16[150,16,3]{0,1,2:T(8,128)(2,1)}, bf16[150,16,3]{0,1,2:T(8,128)(2,1)S(1)}, u32[]{:S(2)}, u32[]{:S(2)}) collective-permute-start(bf16[150,16,3]{0,1,2:T(8,128)(2,1)} %get-tuple-element.198), channel_id=1, source_target_pairs={{1,0},{2,1},{3,2},{0,3},{5,4},{6,5},{7,6},{4,7},{9,8},{10,9},{11,1... | collective-permute-start | bytes 43208 | tf_op jit(solution)/shard_map/ppermute | solution.py:18
  27.4 19.8 %collective-permute-start.3 = (bf16[150,3,262]{2,0,1:T(8,128)(2,1)S(1)}, bf16[150,3,262]{2,0,1:T(8,128)(2,1)}, u32[]{:S(2)}, u32[]{:S(2)}) collective-permute-start(bf16[150,3,262]{2,0,1:T(8,128)(2,1)S(1)} %copy.37), channel_id=1, source_target_pairs={{4,0},{8,4},{12,8},{16,12},{20,16},{24,20},{28,24},{5,1},{9,5},{13... | collective-permute-start | bytes 707408 | tf_op jit(solution)/shard_map/ppermute | solution.py:18
  30.7 17.9 %copy-start.46 = (pred[262]{0:T(512)(128)(4,1)S(1)}, pred[262]{0:T(512)(128)(4,1)}, u32[]{:S(2)}) copy-start(pred[262]{0:T(512)(128)(4,1)} %compare_and_fusion) | copy-start | bytes 790
  43.8 13.3 %collective-permute-start.2 = (bf16[150,3,262]{2,0,1:T(8,128)(2,1)}, bf16[150,3,262]{2,0,1:T(8,128)(2,1)}, u32[]{:S(2)}, u32[]{:S(2)}) collective-permute-start(bf16[150,3,262]{2,0,1:T(8,128)(2,1)} %copy.33), channel_id=1, source_target_pairs={{0,4},{4,8},{8,12},{12,16},{16,20},{20,24},{24,28},{1,5},{5,9},{9,... | collective-permute-start | bytes 707408 | tf_op jit(solution)/shard_map/ppermute | solution.py:16
  58.4 5.5 %copy-start.7 = (f32[150,1,1]{0,2,1:T(1,128)S(1)}, f32[150,1,1]{0,2,1:T(1,128)}, u32[]{:S(2)}) copy-start(f32[150,1,1]{0,2,1:T(1,128)} %get-tuple-element.227) | copy-start | bytes 1804
  58.4 5.5 %copy-start.8 = (f32[150,1,1]{0,2,1:T(1,128)S(1)}, f32[150,1,1]{0,2,1:T(1,128)}, u32[]{:S(2)}) copy-start(f32[150,1,1]{0,2,1:T(1,128)} %get-tuple-element.228) | copy-start | bytes 1804
  58.4 5.5 %copy-start.9 = (f32[150,1,1]{0,2,1:T(1,128)S(1)}, f32[150,1,1]{0,2,1:T(1,128)}, u32[]{:S(2)}) copy-start(f32[150,1,1]{0,2,1:T(1,128)} %get-tuple-element.229) | copy-start | bytes 1804
  58.5 5.5 %copy-start.10 = (f32[150,1,1]{0,2,1:T(1,128)S(1)}, f32[150,1,1]{0,2,1:T(1,128)}, u32[]{:S(2)}) copy-start(f32[150,1,1]{0,2,1:T(1,128)} %get-tuple-element.230) | copy-start | bytes 1804
  58.5 5.5 %copy-start.11 = (f32[150,1,1]{0,2,1:T(1,128)S(1)}, f32[150,1,1]{0,2,1:T(1,128)}, u32[]{:S(2)}) copy-start(f32[150,1,1]{0,2,1:T(1,128)} %get-tuple-element.231) | copy-start | bytes 1804
  58.5 5.5 %copy-start.12 = (f32[150,1,1]{0,2,1:T(1,128)S(1)}, f32[150,1,1]{0,2,1:T(1,128)}, u32[]{:S(2)}) copy-start(f32[150,1,1]{0,2,1:T(1,128)} %get-tuple-element.232) | copy-start | bytes 1804
  58.5 5.5 %copy-start.13 = (f32[150,1,1]{0,2,1:T(1,128)S(1)}, f32[150,1,1]{0,2,1:T(1,128)}, u32[]{:S(2)}) copy-start(f32[150,1,1]{0,2,1:T(1,128)} %get-tuple-element.233) | copy-start | bytes 1804
  58.5 5.5 %copy-start.14 = (f32[150,1,1]{0,2,1:T(1,128)S(1)}, f32[150,1,1]{0,2,1:T(1,128)}, u32[]{:S(2)}) copy-start(f32[150,1,1]{0,2,1:T(1,128)} %get-tuple-element.234) | copy-start | bytes 1804
  58.5 5.5 %copy-start.15 = (f32[150,1,1]{0,2,1:T(1,128)S(1)}, f32[150,1,1]{0,2,1:T(1,128)}, u32[]{:S(2)}) copy-start(f32[150,1,1]{0,2,1:T(1,128)} %get-tuple-element.235) | copy-start | bytes 1804
  58.5 5.5 %copy-start.16 = (f32[150,1,1]{0,2,1:T(1,128)S(1)}, f32[150,1,1]{0,2,1:T(1,128)}, u32[]{:S(2)}) copy-start(f32[150,1,1]{0,2,1:T(1,128)} %get-tuple-element.236) | copy-start | bytes 1804
  58.5 5.5 %copy-start.17 = (f32[150,1,1]{0,2,1:T(1,128)S(1)}, f32[150,1,1]{0,2,1:T(1,128)}, u32[]{:S(2)}) copy-start(f32[150,1,1]{0,2,1:T(1,128)} %get-tuple-element.237) | copy-start | bytes 1804
  58.5 5.5 %copy-start.18 = (f32[150,1,1]{0,2,1:T(1,128)S(1)}, f32[150,1,1]{0,2,1:T(1,128)}, u32[]{:S(2)}) copy-start(f32[150,1,1]{0,2,1:T(1,128)} %get-tuple-element.238) | copy-start | bytes 1804
  58.5 5.5 %copy-start.19 = (f32[150,1,1]{0,2,1:T(1,128)S(1)}, f32[150,1,1]{0,2,1:T(1,128)}, u32[]{:S(2)}) copy-start(f32[150,1,1]{0,2,1:T(1,128)} %get-tuple-element.239) | copy-start | bytes 1804
  58.5 5.5 %copy-start.20 = (f32[150,1,1]{0,2,1:T(1,128)S(1)}, f32[150,1,1]{0,2,1:T(1,128)}, u32[]{:S(2)}) copy-start(f32[150,1,1]{0,2,1:T(1,128)} %get-tuple-element.240) | copy-start | bytes 1804
  58.6 5.5 %copy-start.21 = (f32[150,1,1]{0,2,1:T(1,128)S(1)}, f32[150,1,1]{0,2,1:T(1,128)}, u32[]{:S(2)}) copy-start(f32[150,1,1]{0,2,1:T(1,128)} %get-tuple-element.241) | copy-start | bytes 1804
  58.6 5.5 %copy-start.22 = (f32[150,1,1]{0,2,1:T(1,128)S(1)}, f32[150,1,1]{0,2,1:T(1,128)}, u32[]{:S(2)}) copy-start(f32[150,1,1]{0,2,1:T(1,128)} %get-tuple-element.242) | copy-start | bytes 1804
  58.6 5.5 %copy-start.23 = (f32[150,1,1]{0,2,1:T(1,128)S(1)}, f32[150,1,1]{0,2,1:T(1,128)}, u32[]{:S(2)}) copy-start(f32[150,1,1]{0,2,1:T(1,128)} %get-tuple-element.243) | copy-start | bytes 1804
  58.6 5.5 %copy-start.24 = (f32[150,1,1]{0,2,1:T(1,128)S(1)}, f32[150,1,1]{0,2,1:T(1,128)}, u32[]{:S(2)}) copy-start(f32[150,1,1]{0,2,1:T(1,128)} %get-tuple-element.244) | copy-start | bytes 1804
  58.6 5.5 %copy-start.25 = (f32[150,1,1]{0,2,1:T(1,128)S(1)}, f32[150,1,1]{0,2,1:T(1,128)}, u32[]{:S(2)}) copy-start(f32[150,1,1]{0,2,1:T(1,128)} %get-tuple-element.245) | copy-start | bytes 1804
  58.6 5.5 %copy-start.26 = (f32[150,1,1]{0,2,1:T(1,128)S(1)}, f32[150,1,1]{0,2,1:T(1,128)}, u32[]{:S(2)}) copy-start(f32[150,1,1]{0,2,1:T(1,128)} %get-tuple-element.246) | copy-start | bytes 1804
  58.6 5.5 %copy-start.27 = (f32[150,1,1]{0,2,1:T(1,128)S(1)}, f32[150,1,1]{0,2,1:T(1,128)}, u32[]{:S(2)}) copy-start(f32[150,1,1]{0,2,1:T(1,128)} %get-tuple-element.247) | copy-start | bytes 1804
  58.6 5.5 %copy-start.28 = (f32[150,1,1]{0,2,1:T(1,128)S(1)}, f32[150,1,1]{0,2,1:T(1,128)}, u32[]{:S(2)}) copy-start(f32[150,1,1]{0,2,1:T(1,128)} %get-tuple-element.248) | copy-start | bytes 1804
  58.6 5.5 %copy-start.29 = (f32[150,1,1]{0,2,1:T(1,128)S(1)}, f32[150,1,1]{0,2,1:T(1,128)}, u32[]{:S(2)}) copy-start(f32[150,1,1]{0,2,1:T(1,128)} %get-tuple-element.249) | copy-start | bytes 1804
  58.6 5.5 %copy-start.30 = (f32[150,1,1]{0,2,1:T(1,128)S(1)}, f32[150,1,1]{0,2,1:T(1,128)}, u32[]{:S(2)}) copy-start(f32[150,1,1]{0,2,1:T(1,128)} %get-tuple-element.250) | copy-start | bytes 1804
  58.7 5.5 %copy-start.31 = (f32[150,1,1]{0,2,1:T(1,128)S(1)}, f32[150,1,1]{0,2,1:T(1,128)}, u32[]{:S(2)}) copy-start(f32[150,1,1]{0,2,1:T(1,128)} %get-tuple-element.251) | copy-start | bytes 1804
  58.7 5.5 %copy-start.32 = (f32[150,1,1]{0,2,1:T(1,128)S(1)}, f32[150,1,1]{0,2,1:T(1,128)}, u32[]{:S(2)}) copy-start(f32[150,1,1]{0,2,1:T(1,128)} %get-tuple-element.252) | copy-start | bytes 1804
  58.7 5.5 %copy-start.33 = (f32[150,1,1]{0,2,1:T(1,128)S(1)}, f32[150,1,1]{0,2,1:T(1,128)}, u32[]{:S(2)}) copy-start(f32[150,1,1]{0,2,1:T(1,128)} %get-tuple-element.253) | copy-start | bytes 1804
  58.7 5.5 %copy-start.34 = (f32[150,1,1]{0,2,1:T(1,128)S(1)}, f32[150,1,1]{0,2,1:T(1,128)}, u32[]{:S(2)}) copy-start(f32[150,1,1]{0,2,1:T(1,128)} %get-tuple-element.205) | copy-start | bytes 1804
  58.7 5.5 %copy-start.35 = (f32[150,1,1]{0,2,1:T(1,128)S(1)}, f32[150,1,1]{0,2,1:T(1,128)}, u32[]{:S(2)}) copy-start(f32[150,1,1]{0,2,1:T(1,128)} %get-tuple-element.206) | copy-start | bytes 1804
  58.7 5.5 %copy-start.36 = (f32[150,1,1]{0,2,1:T(1,128)S(1)}, f32[150,1,1]{0,2,1:T(1,128)}, u32[]{:S(2)}) copy-start(f32[150,1,1]{0,2,1:T(1,128)} %get-tuple-element.207) | copy-start | bytes 1804
  58.7 5.5 %copy-start.37 = (f32[150,1,1]{0,2,1:T(1,128)S(1)}, f32[150,1,1]{0,2,1:T(1,128)}, u32[]{:S(2)}) copy-start(f32[150,1,1]{0,2,1:T(1,128)} %get-tuple-element.208) | copy-start | bytes 1804
  58.7 5.5 %copy-start.38 = (f32[150,1,1]{0,2,1:T(1,128)S(1)}, f32[150,1,1]{0,2,1:T(1,128)}, u32[]{:S(2)}) copy-start(f32[150,1,1]{0,2,1:T(1,128)} %get-tuple-element.209) | copy-start | bytes 1804
  58.7 5.5 %copy-start.39 = (f32[150,1,1]{0,2,1:T(1,128)S(1)}, f32[150,1,1]{0,2,1:T(1,128)}, u32[]{:S(2)}) copy-start(f32[150,1,1]{0,2,1:T(1,128)} %get-tuple-element.210) | copy-start | bytes 1804
  58.8 5.5 %copy-start.40 = (f32[150,1,1]{0,2,1:T(1,128)S(1)}, f32[150,1,1]{0,2,1:T(1,128)}, u32[]{:S(2)}) copy-start(f32[150,1,1]{0,2,1:T(1,128)} %get-tuple-element.211) | copy-start | bytes 1804
  105.6 6.3 %copy-start.47 = (bf16[150,600]{1,0:T(8,128)(2,1)S(1)}, bf16[150,600]{1,0:T(8,128)(2,1)}, u32[]{:S(2)}) copy-start(bf16[150,600]{1,0:T(8,128)(2,1)} %param.16) | copy-start | bytes 540004
  105.6 6.3 %copy-start.48 = (f32[150]{0:T(256)S(1)}, f32[150]{0:T(256)}, u32[]{:S(2)}) copy-start(f32[150]{0:T(256)} %param.15) | copy-start | bytes 1804
  128.1 6.6 %copy-start.5 = (f32[2,150,512]{2,0,1:T(2,128)S(1)}, f32[2,150,512]{2,0,1:T(2,128)}, u32[]{:S(2)}) copy-start(f32[2,150,512]{2,0,1:T(2,128)} %param.18) | copy-start | bytes 1843204
  131.0 20.0 %all-to-all-start = ((bf16[150,16,256]{2,0,1:T(8,128)(2,1)}), bf16[150,16,256]{2,0,1:T(8,128)(2,1)S(1)}, u32[]{:S(2)}, u32[]{:S(2)}) async-start(bf16[150,16,256]{2,0,1:T(8,128)(2,1)} %copy.42), calls=%async_computation | async-start | bytes 2490368 | tf_op jit(solution)/shard_map/all_to_all | solution.py:109
  158.9 6.0 %copy-start.2 = (bf16[150,16,256]{2,1,0:T(8,128)(2,1)S(1)}, bf16[150,16,256]{2,1,0:T(8,128)(2,1)}, u32[]{:S(2)}) copy-start(bf16[150,16,256]{2,1,0:T(8,128)(2,1)} %get-tuple-element.144) | copy-start | bytes 3686404
  160.6 20.7 %all-to-all-start.1 = ((bf16[4,150,4,256]{3,2,1,0:T(4,128)(2,1)}), bf16[4,150,4,256]{3,2,1,0:T(4,128)(2,1)}, u32[]{:S(2)}, u32[]{:S(2)}) async-start(bf16[4,150,4,256]{3,2,1,0:T(4,128)(2,1)} %copy.45), calls=%async_computation.1 | async-start | bytes 2457600 | tf_op jit(solution)/shard_map/all_to_all | solution.py:125
  (7 other events, 30.3 us)
